TPU v7x, 32 devices: a whole 2x2x4 slice. The times are simulated.
32 devices in a mesh: groups: 2 (over y), users: 4 (over z), routers: 2 (over x), heads: 2 (over core).
Axes of the slice: x: 2, y: 2, z: 4, core: 2. Of those that a mesh axis runs over, the one named last changes fastest.
Arguments:
- items: bfloat16 [64, 64, 1024], P(('groups', 'users', 'routers')), parts along dimension 0, may hold values from -6 to 6
- block_owner: int32 [64, 1], P(('groups', 'users', 'routers')), parts along dimension 0, may hold values from 0 to 3; in each aligned block of 4 rows (0 to 3, 4 to 7, ...) at most 2 rows name the same one
- block_user: int32 [64], P(('groups', 'users', 'routers')), parts along dimension 0, may hold values from 0 to 1
- block_fill: int32 [64], P(('groups', 'users', 'routers')), parts along dimension 0, may hold values from 1 to 64
- prefix_keys: bfloat16 [16, 256, 1024], P(('groups', 'users'), None, 'heads'), parts along dimension 0, may hold values from -6 to 6
- prefix_values: bfloat16 [16, 256, 1024], P(('groups', 'users'), None, 'heads'), parts along dimension 0, may hold values from -6 to 6
- w_in: bfloat16 [4, 1024, 1024], P(None, 'routers', 'heads'), may hold values from -0.1875 to 0.1875
- attn_gain: bfloat16 [1024], P('heads'), may hold values from 0.25 to 1.75
- w_o: bfloat16 [1024, 1024], P('heads', 'routers'), may hold values from -0.1875 to 0.1875
- mlp_gain: bfloat16 [1024], replicated, may hold values from 0.25 to 1.75
- w_one: bfloat16 [1024, 256], replicated, may hold values from -0.1875 to 0.1875
- w_two: bfloat16 [256], replicated, may hold values from -0.375 to 0.375
Outputs:
- scores: float32 [64, 64], P(('groups', 'users', 'routers')), parts along dimension 0
There are 2 independent parts, one for each index of `groups`. A program takes and returns all parts, laid end to end along the dimension named above; an argument that names none is the same for every part. Nothing has to cross between parts.
Inputs may be any that keep to these rules, and one draw needn't show every extreme that they name: `block_owner`: within the rows of one device (aligned blocks of 4 blocks), no owner is named by more than 2 rows, and in every draw some owner is named by exactly 2 rows of some device.
All inputs are finite; a program needn't handle non-finite values.
Results may differ from a plain program's by a relative error of at most 0.005.
Values may be sent and summed in bfloat16 or wider, within the bound.
A program may use at most 64 MiB of HBM per device.

v0:
```python
import functools
import math

import jax
import jax.numpy as jnp
from jax import lax
from jax.experimental import pallas as pl
from jax.experimental.pallas import tpu as pltpu
from jax.sharding import PartitionSpec as P

HEAD_DIM = 128
CAP = 2
EPSILON = 1e-05
TREE_EIGHTHS = (0, 5, 5, 5, 4)
PARTS = (4, 1, 1, 1, 4)
ORDER = (
    [(0, "g", part) for part in range(PARTS[0])]
    + [(1, "t", 0), (2, "t", 0), (1, "g", 0), (3, "t", 0), (4, "t", 0), (2, "g", 0), (3, "g", 0)]
    + [(4, "g", part) for part in range(PARTS[4])]
)
F32 = jnp.float32
BF16 = jnp.bfloat16
MESH = pl.DeviceIdType.MESH


def silu(v):
    return 0.5 * v * (1.0 + jnp.tanh(0.5 * v))


def scorer(
    sizes,
    items_ref,
    owner_ref,
    user_ref,
    fill_ref,
    keys_ref,
    values_ref,
    w_in_ref,
    attn_gain_ref,
    w_o_ref,
    mlp_gain_ref,
    w_one_ref,
    w_two_ref,
    out_ref,
    items_v,
    out_slots,
    x_all,
    mask_out,
    mask_all,
    keys_v,
    values_v,
    w_all,
    wo_all,
    w_one_v,
    q_v,
    own_v,
    att_v,
    gated_v,
    stat_out,
    stat_in,
    part_out,
    part_own,
    part_in,
    sc_out,
    ret,
    local_sem,
    z_send,
    z_recv,
    m_send,
    m_recv,
    rel_send,
    rel_recv,
    x_send,
    x_recv,
    y_send,
    y_recv,
    w_send,
    w_recv,
    st_sem,
    po_send,
    po_recv,
    sc_send,
    sc_recv,
):
    groups, users, routers, heads = sizes
    g = lax.axis_index("groups")
    me = lax.axis_index("users")
    r = lax.axis_index("routers")
    h = lax.axis_index("heads")
    mate = 1 - h
    blocks, width, model = items_v.shape
    slots = x_all.shape[0]
    half_width = q_v.shape[1]
    heads_here = half_width // HEAD_DIM
    hd_all = half_width * heads
    rows = slots * width
    depth = w_all.shape[2]
    out_cols = wo_all.shape[2]
    wh = width // heads
    scale = HEAD_DIM ** (-0.5)
    positions = keys_v.shape[0] * keys_v.shape[1]
    per_user = keys_v.shape[1]

    c_items = pltpu.make_async_copy(items_ref, items_v, local_sem.at[0])
    c_items.start()

    barrier = pltpu.get_barrier_semaphore()
    count = 0
    for j in range(1, routers):
        pl.semaphore_signal(
            barrier, inc=1, device_id={"routers": lax.rem(r + j, routers)}, device_id_type=MESH
        )
        count += 1
    for i in range(1, groups):
        pl.semaphore_signal(
            barrier, inc=1, device_id={"groups": lax.rem(g + i, groups)}, device_id_type=MESH
        )
        count += 1
    pl.semaphore_signal(barrier, inc=1, device_id={"heads": mate}, device_id_type=MESH)
    count += 1
    for k in range(1, users):
        for e in range(heads):
            pl.semaphore_signal(
                barrier,
                inc=1,
                device_id={"users": lax.rem(me + k, users), "heads": e},
                device_id_type=MESH,
            )
            count += 1
    c_keys = pltpu.make_async_copy(keys_ref, keys_v, local_sem.at[1])
    c_values = pltpu.make_async_copy(values_ref, values_v, local_sem.at[2])
    c_win = pltpu.make_async_copy(w_in_ref, w_all.at[:, r], local_sem.at[3])
    c_wo = pltpu.make_async_copy(w_o_ref, wo_all.at[r], local_sem.at[4])
    c_one = pltpu.make_async_copy(w_one_ref, w_one_v, local_sem.at[5])
    pl.semaphore_wait(barrier, count)

    pieces = ORDER
    number = {piece: t for t, piece in enumerate(pieces)}
    parity = lax.rem(me, 2)
    pair = me + 1 - 2 * parity

    def piece_rows(p, kind, part, owner_group, owner_parity):
        length = depth if p < 4 else half_width
        tree = length * TREE_EIGHTHS[p] // 8 // (2 * groups) // 16 * 16
        if kind == "t":
            return pl.ds(pl.multiple_of((owner_group * 2 + owner_parity) * tree, tree), tree)
        direct = length // groups - 2 * tree
        share = direct // PARTS[p]
        start = 2 * groups * tree + owner_group * direct + part * share
        return pl.ds(pl.multiple_of(start, math.gcd(share, 16)), share)

    def weight_slot(owner_router, owner_group, owner_parity, t):
        p, kind, part = pieces[t]
        span = piece_rows(p, kind, part, owner_group, owner_parity)
        if p < 4:
            return w_all.at[p, owner_router, span, :]
        return wo_all.at[owner_router, span, :]

    def x_copy(j, t, source_router):
        p, kind, part = pieces[t]
        span = piece_rows(p, kind, part, g, parity)
        src = w_in_ref.at[p, span, :] if p < 4 else w_o_ref.at[span, :]
        return pltpu.make_async_remote_copy(
            src_ref=src,
            dst_ref=weight_slot(source_router, g, parity, t),
            send_sem=x_send.at[j, t],
            recv_sem=x_recv.at[j, t],
            device_id={"routers": lax.rem(r + j, routers)},
            device_id_type=MESH,
        )

    def y_copy(i, j, t, owner_group):
        spot = weight_slot(lax.rem(r - j + routers, routers), owner_group, parity, t)
        return pltpu.make_async_remote_copy(
            src_ref=spot,
            dst_ref=spot,
            send_sem=y_send.at[i, j, t],
            recv_sem=y_recv.at[i, j, t],
            device_id={"groups": lax.rem(g + i, groups)},
            device_id_type=MESH,
        )

    def pair_copy(i, j, p, owner_parity):
        spot = weight_slot(
            lax.rem(r - j + routers, routers),
            lax.rem(g - i + groups, groups),
            owner_parity,
            number[p, "t", 0],
        )
        return pltpu.make_async_remote_copy(
            src_ref=spot,
            dst_ref=spot,
            send_sem=w_send.at[i, j, p],
            recv_sem=w_recv.at[i, j, p],
            device_id={"users": pair},
            device_id_type=MESH,
        )

    for t in range(len(pieces)):
        for j in range(1, routers):
            x_copy(j, t, r).start()
    for c in (c_win, c_keys, c_values, c_wo, c_one):
        c.start()

    owners = [owner_ref[b] for b in range(blocks)]
    ranks = []
    for b in range(blocks):
        rank = jnp.int32(0)
        for a in range(b):
            rank = rank + jnp.where(owners[a] == owners[b], 1, 0)
        ranks.append(rank)

    def slot_source(dest, cap):
        index, user = jnp.int32(0), jnp.int32(-1)
        for b in range(blocks):
            hit = (owners[b] == dest) & (ranks[b] == cap)
            index = jnp.where(hit, b, index)
            user = jnp.where(hit, user_ref[b], user)
        return index, user

    lane_user = lax.broadcasted_iota(jnp.int32, (1, positions), 1) // per_user
    mask_copies, item_copies = {}, {}

    def z_copy(k, source):
        return pltpu.make_async_remote_copy(
            src_ref=out_slots.at[k],
            dst_ref=x_all.at[pl.ds(source * CAP, CAP), pl.ds(pl.multiple_of(h * wh, wh), wh), :],
            send_sem=z_send.at[k],
            recv_sem=z_recv.at[k],
            device_id={"users": lax.rem(me + k, users)},
            device_id_type=MESH,
        )

    def m_copy(k, source):
        return pltpu.make_async_remote_copy(
            src_ref=mask_out.at[k],
            dst_ref=mask_all.at[source],
            send_sem=m_send.at[k],
            recv_sem=m_recv.at[k],
            device_id={"users": lax.rem(me + k, users)},
            device_id_type=MESH,
        )

    def relay_copy(k, part):
        source = lax.rem(me - k + users, users)
        spot = x_all.at[pl.ds(source * CAP, CAP), pl.ds(pl.multiple_of(part * wh, wh), wh), :]
        return pltpu.make_async_remote_copy(
            src_ref=spot,
            dst_ref=spot,
            send_sem=rel_send.at[k],
            recv_sem=rel_recv.at[k],
            device_id={"heads": mate},
            device_id_type=MESH,
        )

    c_items.wait()
    for k in list(range(1, users)) + [0]:
        dest = lax.rem(me + k, users)
        for cap in range(CAP):
            index, user = slot_source(dest, cap)
            line = jnp.where(lane_user == user, 1.0, 0.0).astype(F32)
            if k == 0:
                x_all[me * CAP + cap] = items_v[index]
                mask_all[me, cap : cap + 1, :] = line
            else:
                out_slots[k, cap] = items_v[index, pl.ds(pl.multiple_of(h * wh, wh), wh), :]
                mask_out[k, cap : cap + 1, :] = line
        if k:
            z_copy(k, me).start()
            m_copy(k, me).start()

    def forward(p, kind, part=0):
        t = number[p, kind, part]
        for j in range(1, routers):
            x_copy(j, t, lax.rem(r - j + routers, routers)).wait_recv()
            for i in range(1, groups):
                y_copy(i, j, t, g).start()
            if kind == "t":
                pair_copy(0, j, p, parity).start()

    def y_landed(p, kind, part=0):
        t = number[p, kind, part]
        for j in range(1, routers):
            for i in range(1, groups):
                y_copy(i, j, t, lax.rem(g - i + groups, groups)).wait_recv()
                if kind == "t":
                    pair_copy(i, j, p, parity).start()

    def landed(p):
        for part in range(PARTS[p]):
            y_landed(p, "g", part)
        if TREE_EIGHTHS[p]:
            for j in range(1, routers):
                for i in range(groups):
                    pair_copy(i, j, p, 1 - parity).wait_recv()

    tile_slots = 4
    tile = tile_slots * width
    tiles = rows // tile

    def x_tile(i):
        return x_all[pl.ds(i * tile_slots, tile_slots)].reshape(tile, model)

    def span_of(i):
        return pl.ds(pl.multiple_of(i * tile, tile), tile)

    def projected(p, i):
        x = x_tile(i)
        total = jnp.zeros((tile, half_width), F32)
        for a in range(routers):
            total = total + jnp.dot(
                x[:, a * depth : (a + 1) * depth], w_all[p, a], preferred_element_type=F32
            )
        return silu(total)

    def query(i):
        q_v[span_of(i), :] = projected(0, i).astype(BF16)

    def attend(i):
        span = span_of(i)
        for e in range(heads_here):
            cols = slice(e * HEAD_DIM, (e + 1) * HEAD_DIM)
            raw = lax.dot_general(
                q_v[span, cols],
                keys_v[:, :, cols].reshape(positions, HEAD_DIM),
                (((1,), (1,)), ((), ())),
                preferred_element_type=F32,
            )
            weights = silu(raw * scale)
            parts = []
            for s in range(tile_slots):
                line = mask_all[i * (tile_slots // CAP) + s // CAP, s % CAP : s % CAP + 1, :]
                parts.append(weights[s * width : (s + 1) * width] * line)
            weights = jnp.concatenate(parts, axis=0).astype(BF16)
            att_v[span, cols] = (
                jnp.dot(
                    weights,
                    values_v[:, :, cols].reshape(positions, HEAD_DIM),
                    preferred_element_type=F32,
                )
                .astype(BF16)
                .astype(F32)
            )

    def self_key(i):
        span = span_of(i)
        keys = projected(1, i)
        for e in range(heads_here):
            cols = slice(e * HEAD_DIM, (e + 1) * HEAD_DIM)
            own = jnp.sum(q_v[span, cols].astype(F32) * keys[:, cols], axis=1, keepdims=True)
            own_v[span, cols] = jnp.broadcast_to(silu(own * scale), (tile, HEAD_DIM))

    lane = lax.broadcasted_iota(jnp.int32, (tile, 128), 1)

    def self_value(i):
        span = span_of(i)
        att = att_v[span, :] + own_v[span, :] * projected(2, i)
        att_v[span, :] = att
        total = jnp.sum(att, axis=1, keepdims=True)
        square = jnp.sum(att * att, axis=1, keepdims=True)
        stat_out[span, :] = jnp.where(lane == 0, total, square)

    def gate(i):
        span = span_of(i)
        both = stat_out[span, :] + stat_in[span, :]
        mean = both[:, 0:1] / hd_all
        var = both[:, 1:2] / hd_all - mean * mean
        gated_v[span, :] = (
            (att_v[span, :] - mean)
            * lax.rsqrt(var + EPSILON)
            * attn_gain_ref[...].astype(F32).reshape(1, -1)
            * projected(3, i)
        ).astype(BF16)

    with jax.named_scope("fwd0"):
        for part in range(PARTS[0]):
            forward(0, "g", part)
    with jax.named_scope("fwd1"):
        forward(1, "t")
        forward(2, "t")
        forward(1, "g")
    with jax.named_scope("items"):
        for k in range(1, users):
            z_copy(k, lax.rem(me - k + users, users)).wait_recv()
            relay_copy(k, h).start()
    with jax.named_scope("fwd1b"):
        y_landed(1, "t")
    with jax.named_scope("items2"):
        for k in range(1, users):
            m_copy(k, lax.rem(me - k + users, users)).wait_recv()
            relay_copy(k, mate).wait_recv()
        c_win.wait()
    with jax.named_scope("land0"):
        landed(0)
    with jax.named_scope("query"):
        pl.loop(0, tiles)(query)
    with jax.named_scope("fwd3a"):
        forward(3, "t")
        y_landed(2, "t")
    c_keys.wait()
    c_values.wait()
    with jax.named_scope("attend0"):
        pl.loop(0, tiles // 2)(attend)
    with jax.named_scope("fwd4a"):
        forward(4, "t")
    with jax.named_scope("attend1"):
        pl.loop(tiles // 2, tiles)(attend)
    with jax.named_scope("fwd2b"):
        forward(2, "g")
    with jax.named_scope("land1"):
        landed(1)
    with jax.named_scope("key"):
        pl.loop(0, tiles)(self_key)
    with jax.named_scope("fwd3b"):
        forward(3, "g")
        y_landed(3, "t")
        forward(4, "g", 0)
        y_landed(4, "t")
        forward(4, "g", 1)
    with jax.named_scope("land2"):
        landed(2)
    with jax.named_scope("value0"):
        pl.loop(0, tiles // 2)(self_value)
    with jax.named_scope("fwd4c"):
        forward(4, "g", 2)
    with jax.named_scope("value1"):
        pl.loop(tiles // 2, tiles)(self_value)

    stat_copy = pltpu.make_async_remote_copy(
        src_ref=stat_out,
        dst_ref=stat_in,
        send_sem=st_sem.at[0],
        recv_sem=st_sem.at[1],
        device_id={"heads": mate},
        device_id_type=MESH,
    )
    stat_copy.start()
    with jax.named_scope("fwd4b"):
        forward(4, "g", 3)
    with jax.named_scope("land3"):
        landed(3)
    with jax.named_scope("statwait"):
        stat_copy.wait_recv()
    with jax.named_scope("gate"):
        pl.loop(0, tiles)(gate)

    half = rows // heads
    c_wo.wait()

    mine = users // heads
    piece = half // 2
    source_rows = CAP * width

    def far_first(e, i, amount):
        return jnp.where(me < e * mine + mine // 2, amount - 1 - i, i)

    def part_copy(j, c):
        spot = pl.ds(pl.multiple_of(c * piece, piece), piece)
        return pltpu.make_async_remote_copy(
            src_ref=part_out.at[j, spot, :],
            dst_ref=part_in.at[j, spot, :],
            send_sem=po_send.at[j, c],
            recv_sem=po_recv.at[j, c],
            device_id={"heads": mate},
            device_id_type=MESH,
        )

    def out_project(j, row_half, c, target):
        src = pl.ds(pl.multiple_of(row_half * half + c * piece, piece), piece)
        target[j, pl.ds(pl.multiple_of(c * piece, piece), piece), :] = jnp.dot(
            gated_v[src, :],
            wo_all[lax.rem(r - j + routers, routers)],
            preferred_element_type=F32,
        ).astype(target.dtype)

    def shares(j):
        for i in range(2):
            c = far_first(mate, i, 2)
            out_project(j, mate, c, part_out)
            part_copy(j, c).start()

    with jax.named_scope("outown"):
        shares(0)
        for c in range(2):
            out_project(0, h, c, part_own)
    with jax.named_scope("land4"):
        landed(4)
    for j in range(1, routers):
        shares(j)
    for j in range(1, routers):
        for c in range(2):
            out_project(j, h, c, part_own)
    c_one.wait()

    two = jnp.broadcast_to(
        w_two_ref[...].astype(F32).reshape(1, -1), (8, w_two_ref.shape[0])
    ).astype(BF16)

    def score(source, i):
        span = pl.ds(pl.multiple_of(source * source_rows, source_rows), source_rows)
        x = x_all[pl.ds((h * mine + source) * CAP, CAP)].reshape(source_rows, model).astype(F32)
        mixed = []
        for a in range(routers):
            j = lax.rem(r - a + routers, routers)
            mixed.append(part_own[j, span, :] + part_in[j, span, :].astype(F32))
        residual = x + jnp.concatenate(mixed, axis=1)
        norm = lax.rsqrt(jnp.sum(residual * residual, axis=1, keepdims=True) / model + EPSILON)
        normed = (residual * norm * mlp_gain_ref[...].astype(F32).reshape(1, -1)).astype(BF16)
        hidden = silu(jnp.dot(normed, w_one_v[...], preferred_element_type=F32)).astype(BF16)
        sc_out[i] = lax.dot_general(
            two, hidden, (((1,), (1,)), ((), ())), preferred_element_type=F32
        )

    def score_copy(i, e, owner, sem):
        return pltpu.make_async_remote_copy(
            src_ref=sc_out.at[i],
            dst_ref=ret.at[owner],
            send_sem=sc_send.at[i, e],
            recv_sem=sc_recv.at[sem],
            device_id={"users": h * mine + far_first(h, i, mine), "heads": e},
            device_id_type=MESH,
        )

    for i in range(mine):
        source = far_first(h, i, mine)
        if i % (mine // 2) == 0:
            with jax.named_scope("partwait"):
                for j in range(routers):
                    part_copy(j, far_first(h, i // (mine // 2), 2)).wait_recv()
        score(source, i)
        target = h * mine + source
        for e in range(heads):
            itself = (target == me) & (h == e)

            @pl.when(jnp.logical_not(itself))
            def _():
                score_copy(i, e, me, me).start()

            @pl.when(itself)
            def _():
                ret[me] = sc_out[i]

    handler = me // mine
    with jax.named_scope("scorewait"):
        for d in range(users):

            @pl.when(jnp.logical_not((d == me) & (h == handler)))
            def _():
                score_copy(0, 0, d, d).wait_recv()

    position = lax.broadcasted_iota(jnp.int32, (1, width), 1)
    for b in range(blocks):
        tile_in = ret[owners[b]]
        line = tile_in[0:1, 0:width]
        for cap in range(1, CAP):
            line = jnp.where(ranks[b] == cap, tile_in[0:1, cap * width : (cap + 1) * width], line)
        out_ref[b : b + 1, :] = jnp.where(position < fill_ref[b], line, 0.0)

    for t in range(len(pieces)):
        for j in range(1, routers):
            x_copy(j, t, r).wait_send()
            for i in range(1, groups):
                y_copy(i, j, t, g).wait_send()
    for p in range(5):
        if TREE_EIGHTHS[p]:
            for j in range(1, routers):
                for i in range(groups):
                    pair_copy(i, j, p, parity).wait_send()
    for k in range(1, users):
        z_copy(k, me).wait_send()
        m_copy(k, me).wait_send()
        relay_copy(k, h).wait_send()
    stat_copy.wait_send()
    for j in range(routers):
        for c in range(2):
            part_copy(j, c).wait_send()
    for i in range(mine):
        for e in range(heads):

            @pl.when(jnp.logical_not((h * mine + far_first(h, i, mine) == me) & (h == e)))
            def _():
                score_copy(i, e, me, me).wait_send()


def local(
    sizes,
    items,
    block_owner,
    block_user,
    block_fill,
    prefix_keys,
    prefix_values,
    w_in,
    attn_gain,
    w_o,
    mlp_gain,
    w_one,
    w_two,
):
    groups, users, routers, heads = sizes
    blocks, width, model = items.shape
    projections, depth, half_width = w_in.shape
    slots = users * CAP
    rows = slots * width
    half = rows // heads
    out_cols = w_o.shape[1]
    cached, per_user, _ = prefix_keys.shape
    positions = cached * per_user
    pieces = len(ORDER)
    dma = pltpu.SemaphoreType.DMA
    hbm = pl.BlockSpec(memory_space=pl.ANY)
    vmem = pl.BlockSpec(memory_space=pltpu.VMEM)
    smem = pl.BlockSpec(memory_space=pltpu.SMEM)
    scratch = [
        pltpu.VMEM((blocks, width, model), BF16),
        pltpu.VMEM((users, CAP, width // heads, model), BF16),
        pltpu.VMEM((slots, width, model), BF16),
        pltpu.VMEM((users, 8, positions), F32),
        pltpu.VMEM((users, 8, positions), F32),
        pltpu.VMEM(prefix_keys.shape, BF16),
        pltpu.VMEM(prefix_values.shape, BF16),
        pltpu.VMEM((projections, routers, depth, half_width), BF16),
        pltpu.VMEM((routers, half_width, out_cols), BF16),
        pltpu.VMEM(w_one.shape, BF16),
        pltpu.VMEM((rows, half_width), BF16),
        pltpu.VMEM((rows, half_width), F32),
        pltpu.VMEM((rows, half_width), F32),
        pltpu.VMEM((rows, half_width), BF16),
        pltpu.VMEM((rows, 128), F32),
        pltpu.VMEM((rows, 128), F32),
        pltpu.VMEM((routers, half, out_cols), BF16),
        pltpu.VMEM((routers, half, out_cols), F32),
        pltpu.VMEM((routers, half, out_cols), BF16),
        pltpu.VMEM((users // heads, 8, CAP * width), F32),
        pltpu.VMEM((users, 8, CAP * width), F32),
        dma((6,)),
        dma((users,)),
        dma((users,)),
        dma((users,)),
        dma((users,)),
        dma((users,)),
        dma((users,)),
        dma((routers, pieces)),
        dma((routers, pieces)),
        dma((groups, routers, pieces)),
        dma((groups, routers, pieces)),
        dma((groups, routers, 5)),
        dma((groups, routers, 5)),
        dma((2,)),
        dma((routers, 2)),
        dma((routers, 2)),
        dma((users // heads, heads)),
        dma((users,)),
    ]
    return pl.pallas_call(
        functools.partial(scorer, sizes),
        out_shape=jax.ShapeDtypeStruct((blocks, width), F32),
        in_specs=[hbm, smem, smem, smem, hbm, hbm, hbm, vmem, hbm, vmem, hbm, vmem],
        out_specs=vmem,
        scratch_shapes=scratch,
        compiler_params=pltpu.CompilerParams(
            collective_id=0, has_side_effects=True, vmem_limit_bytes=62 * 1024 * 1024
        ),
    )(
        items,
        block_owner.reshape(-1),
        block_user,
        block_fill,
        prefix_keys,
        prefix_values,
        w_in,
        attn_gain,
        w_o,
        mlp_gain,
        w_one,
        w_two,
    )


def solution(mesh):
    placed = (
        P(("groups", "users", "routers"), None, None),
        P(("groups", "users", "routers"), None),
        P(("groups", "users", "routers")),
        P(("groups", "users", "routers")),
        P(("groups", "users"), None, "heads"),
        P(("groups", "users"), None, "heads"),
        P(None, "routers", "heads"),
        P("heads"),
        P("heads", "routers"),
        P(),
        P(),
        P(),
    )
    sizes = tuple(mesh.shape[name] for name in ("groups", "users", "routers", "heads"))
    return jax.shard_map(
        functools.partial(local, sizes),
        mesh=mesh,
        in_specs=placed,
        out_specs=P(("groups", "users", "routers"), None),
        check_vma=False,
    )
```

profile of v0, /device:TPU:0, one launch (start us, length us, event | category | flops | bytes accessed | tf_op | source)
XLA Modules:
  0.0 44.6 jit_solution(1481759475760965565)
XLA Ops:
  0.0 43.4 %shard_map.118 = f32[4,64]{1,0:T(4,128)} custom-call(bf16[4,64,1024]{2,1,0:T(8,128)(2,1)} %items_ref.1, s32[4]{0:T(128)} %bitcast.1, s32[4]{0:T(128)} %user_ref.1, s32[4]{0:T(128)} %fill_ref.1, bf16[2,256,512]{2,1,0:T(8,128)(2,1)} %keys_ref.1, bf16[2,256,512]{2,1,0:T(8,128)(2,1)} %values_ref.1, bf16[4,512,512]{2,1,0:T(8,128)(2,1)} %w_in_ref.1, ...), custom_call_target="tpu_custom_call" | custom-call | tf_op jit(solution)/shard_map/pallas_call | solution.py:655
  43.4 1.3 %copy.14 = f32[4,64]{1,0:T(4,128)} copy(f32[4,64]{1,0:T(4,128)} %shard_map.118) | data formatting | bytes 2048
where the time goes:
time: 44.8 us; the launch traced here: 44.6 us
  Pallas kernels  43.4 us (97%)
  local copies, waits for them, and re-layouts  1.26 us (3%)
    pallas_call x1, Pallas kernels, local(): pl.pallas_call(functools.partial(scorer, sizes), out_shape=jax.ShapeDtype...  43.4 us
    unnamed x1, local copies, waits for them, and re-layouts  1.26 us

commit v1 on v0

--- a/solution.py
+++ b/solution.py
@@ -30,18 +30,24 @@
 def scorer(
     sizes,
     items_ref,
+    owner_hbm,
+    user_hbm,
+    fill_hbm,
+    keys_ref,
+    values_ref,
+    w_in_ref,
+    attn_gain_hbm,
+    w_o_ref,
+    mlp_gain_hbm,
+    w_one_ref,
+    w_two_hbm,
+    out_ref,
     owner_ref,
     user_ref,
     fill_ref,
-    keys_ref,
-    values_ref,
-    w_in_ref,
     attn_gain_ref,
-    w_o_ref,
     mlp_gain_ref,
-    w_one_ref,
     w_two_ref,
-    out_ref,
     items_v,
     out_slots,
     x_all,
@@ -64,23 +70,16 @@
     sc_out,
     ret,
     local_sem,
-    z_send,
+    sent,
     z_recv,
-    m_send,
-    m_recv,
-    rel_send,
-    rel_recv,
-    x_send,
+    group_recv,
     x_recv,
-    y_send,
     y_recv,
-    w_send,
     w_recv,
-    st_sem,
-    po_send,
     po_recv,
     sc_send,
     sc_recv,
+    yard,
 ):
     groups, users, routers, heads = sizes
     g = lax.axis_index("groups")
@@ -101,9 +100,6 @@
     positions = keys_v.shape[0] * keys_v.shape[1]
     per_user = keys_v.shape[1]
 
-    c_items = pltpu.make_async_copy(items_ref, items_v, local_sem.at[0])
-    c_items.start()
-
     barrier = pltpu.get_barrier_semaphore()
     count = 0
     for j in range(1, routers):
@@ -127,15 +123,52 @@
                 device_id_type=MESH,
             )
             count += 1
-    c_keys = pltpu.make_async_copy(keys_ref, keys_v, local_sem.at[1])
-    c_values = pltpu.make_async_copy(values_ref, values_v, local_sem.at[2])
-    c_win = pltpu.make_async_copy(w_in_ref, w_all.at[:, r], local_sem.at[3])
-    c_wo = pltpu.make_async_copy(w_o_ref, wo_all.at[r], local_sem.at[4])
-    c_one = pltpu.make_async_copy(w_one_ref, w_one_v, local_sem.at[5])
+    first = [
+        pltpu.make_async_copy(src, dst, local_sem.at[n])
+        for n, (src, dst) in enumerate(
+            (
+                (owner_hbm, owner_ref),
+                (user_hbm, user_ref),
+                (fill_hbm, fill_ref),
+                (items_ref, items_v),
+            )
+        )
+    ]
+    gains = [
+        pltpu.make_async_copy(src, dst, local_sem.at[4 + n])
+        for n, (src, dst) in enumerate(
+            (
+                (attn_gain_hbm, attn_gain_ref),
+                (mlp_gain_hbm, mlp_gain_ref),
+                (w_two_hbm, w_two_ref),
+            )
+        )
+    ]
+    bulk = [
+        pltpu.make_async_copy(src, dst, local_sem.at[7])
+        for src, dst in (
+            (w_in_ref, w_all.at[:, r]),
+            (keys_ref, keys_v),
+            (values_ref, values_v),
+            (w_o_ref, wo_all.at[r]),
+            (w_one_ref, w_one_v),
+        )
+    ]
+
+    def size(*refs):
+        return sum(math.prod(ref.shape) * jnp.dtype(ref.dtype).itemsize for ref in refs)
+
+    def drain(sem, amount):
+        part = yard.at[pl.ds(0, amount // (yard.shape[1] * 2)), :]
+        pltpu.make_async_copy(part, part, sem).wait()
+
+    for c in first:
+        c.start()
     pl.semaphore_wait(barrier, count)
 
     pieces = ORDER
     number = {piece: t for t, piece in enumerate(pieces)}
+    slot_y = [p if kind == "g" else 4 + p for p, kind, _ in pieces]
     parity = lax.rem(me, 2)
     pair = me + 1 - 2 * parity
 
@@ -156,6 +189,15 @@
             return w_all.at[p, owner_router, span, :]
         return wo_all.at[owner_router, span, :]
 
+    def piece_bytes(t):
+        p, kind, part = pieces[t]
+        row = size(w_all) // (4 * routers * depth) if p < 4 else size(wo_all) // (routers * half_width)
+        length = depth if p < 4 else half_width
+        tree = length * TREE_EIGHTHS[p] // 8 // (2 * groups) // 16 * 16
+        if kind == "t":
+            return tree * row
+        return (length // groups - 2 * tree) // PARTS[p] * row
+
     def x_copy(j, t, source_router):
         p, kind, part = pieces[t]
         span = piece_rows(p, kind, part, g, parity)
@@ -163,8 +205,8 @@
         return pltpu.make_async_remote_copy(
             src_ref=src,
             dst_ref=weight_slot(source_router, g, parity, t),
-            send_sem=x_send.at[j, t],
-            recv_sem=x_recv.at[j, t],
+            send_sem=sent.at[0],
+            recv_sem=x_recv.at[j - 1, t],
             device_id={"routers": lax.rem(r + j, routers)},
             device_id_type=MESH,
         )
@@ -174,8 +216,8 @@
         return pltpu.make_async_remote_copy(
             src_ref=spot,
             dst_ref=spot,
-            send_sem=y_send.at[i, j, t],
-            recv_sem=y_recv.at[i, j, t],
+            send_sem=sent.at[0],
+            recv_sem=y_recv.at[i - 1, j - 1, slot_y[t]],
             device_id={"groups": lax.rem(g + i, groups)},
             device_id_type=MESH,
         )
@@ -190,8 +232,8 @@
         return pltpu.make_async_remote_copy(
             src_ref=spot,
             dst_ref=spot,
-            send_sem=w_send.at[i, j, p],
-            recv_sem=w_recv.at[i, j, p],
+            send_sem=sent.at[0],
+            recv_sem=w_recv.at[j - 1, p],
             device_id={"users": pair},
             device_id_type=MESH,
         )
@@ -199,9 +241,11 @@
     for t in range(len(pieces)):
         for j in range(1, routers):
             x_copy(j, t, r).start()
-    for c in (c_win, c_keys, c_values, c_wo, c_one):
+    for c in bulk + gains:
         c.start()
 
+    for c in first[:3]:
+        c.wait()
     owners = [owner_ref[b] for b in range(blocks)]
     ranks = []
     for b in range(blocks):
@@ -218,6 +262,8 @@
             user = jnp.where(hit, user_ref[b], user)
         return index, user
 
+    mask_bytes = size(mask_out) // users
+    slot_bytes = size(out_slots) // users
     lane_user = lax.broadcasted_iota(jnp.int32, (1, positions), 1) // per_user
     mask_copies, item_copies = {}, {}
 
@@ -225,8 +271,8 @@
         return pltpu.make_async_remote_copy(
             src_ref=out_slots.at[k],
             dst_ref=x_all.at[pl.ds(source * CAP, CAP), pl.ds(pl.multiple_of(h * wh, wh), wh), :],
-            send_sem=z_send.at[k],
-            recv_sem=z_recv.at[k],
+            send_sem=sent.at[0],
+            recv_sem=z_recv.at[k - 1],
             device_id={"users": lax.rem(me + k, users)},
             device_id_type=MESH,
         )
@@ -235,8 +281,8 @@
         return pltpu.make_async_remote_copy(
             src_ref=mask_out.at[k],
             dst_ref=mask_all.at[source],
-            send_sem=m_send.at[k],
-            recv_sem=m_recv.at[k],
+            send_sem=sent.at[0],
+            recv_sem=group_recv.at[0],
             device_id={"users": lax.rem(me + k, users)},
             device_id_type=MESH,
         )
@@ -247,13 +293,13 @@
         return pltpu.make_async_remote_copy(
             src_ref=spot,
             dst_ref=spot,
-            send_sem=rel_send.at[k],
-            recv_sem=rel_recv.at[k],
+            send_sem=sent.at[0],
+            recv_sem=group_recv.at[1],
             device_id={"heads": mate},
             device_id_type=MESH,
         )
 
-    c_items.wait()
+    first[3].wait()
     for k in list(range(1, users)) + [0]:
         dest = lax.rem(me + k, users)
         for cap in range(CAP):
@@ -278,21 +324,19 @@
             if kind == "t":
                 pair_copy(0, j, p, parity).start()
 
-    def y_landed(p, kind, part=0):
-        t = number[p, kind, part]
+    def y_landed(p, kind):
+        t = number[p, kind, 0]
         for j in range(1, routers):
             for i in range(1, groups):
                 y_copy(i, j, t, lax.rem(g - i + groups, groups)).wait_recv()
-                if kind == "t":
-                    pair_copy(i, j, p, parity).start()
+                pair_copy(i, j, p, parity).start()
 
     def landed(p):
-        for part in range(PARTS[p]):
-            y_landed(p, "g", part)
-        if TREE_EIGHTHS[p]:
-            for j in range(1, routers):
-                for i in range(groups):
-                    pair_copy(i, j, p, 1 - parity).wait_recv()
+        for j in range(1, routers):
+            for i in range(1, groups):
+                drain(y_recv.at[i - 1, j - 1, p], PARTS[p] * piece_bytes(number[p, "g", 0]))
+            if TREE_EIGHTHS[p]:
+                drain(w_recv.at[j - 1, p], groups * piece_bytes(number[p, "t", 0]))
 
     tile_slots = 4
     tile = tile_slots * width
@@ -386,10 +430,11 @@
     with jax.named_scope("fwd1b"):
         y_landed(1, "t")
     with jax.named_scope("items2"):
-        for k in range(1, users):
-            m_copy(k, lax.rem(me - k + users, users)).wait_recv()
-            relay_copy(k, mate).wait_recv()
-        c_win.wait()
+        drain(group_recv.at[0], (users - 1) * mask_bytes)
+        drain(group_recv.at[1], (users - 1) * slot_bytes)
+        drain(local_sem.at[7], size(w_in_ref, keys_ref, values_ref, w_o_ref, w_one_ref))
+        for c in gains:
+            c.wait()
     with jax.named_scope("land0"):
         landed(0)
     with jax.named_scope("query"):
@@ -397,8 +442,6 @@
     with jax.named_scope("fwd3a"):
         forward(3, "t")
         y_landed(2, "t")
-    c_keys.wait()
-    c_values.wait()
     with jax.named_scope("attend0"):
         pl.loop(0, tiles // 2)(attend)
     with jax.named_scope("fwd4a"):
@@ -429,8 +472,8 @@
     stat_copy = pltpu.make_async_remote_copy(
         src_ref=stat_out,
         dst_ref=stat_in,
-        send_sem=st_sem.at[0],
-        recv_sem=st_sem.at[1],
+        send_sem=sent.at[0],
+        recv_sem=group_recv.at[2],
         device_id={"heads": mate},
         device_id_type=MESH,
     )
@@ -445,7 +488,6 @@
         pl.loop(0, tiles)(gate)
 
     half = rows // heads
-    c_wo.wait()
 
     mine = users // heads
     piece = half // 2
@@ -459,8 +501,8 @@
         return pltpu.make_async_remote_copy(
             src_ref=part_out.at[j, spot, :],
             dst_ref=part_in.at[j, spot, :],
-            send_sem=po_send.at[j, c],
-            recv_sem=po_recv.at[j, c],
+            send_sem=sent.at[0],
+            recv_sem=po_recv.at[c],
             device_id={"heads": mate},
             device_id_type=MESH,
         )
@@ -490,7 +532,6 @@
     for j in range(1, routers):
         for c in range(2):
             out_project(j, h, c, part_own)
-    c_one.wait()
 
     two = jnp.broadcast_to(
         w_two_ref[...].astype(F32).reshape(1, -1), (8, w_two_ref.shape[0])
@@ -525,8 +566,7 @@
         source = far_first(h, i, mine)
         if i % (mine // 2) == 0:
             with jax.named_scope("partwait"):
-                for j in range(routers):
-                    part_copy(j, far_first(h, i // (mine // 2), 2)).wait_recv()
+                drain(po_recv.at[far_first(h, i // (mine // 2), 2)], size(part_in) // 2)
         score(source, i)
         target = h * mine + source
         for e in range(heads):
@@ -540,6 +580,10 @@
             def _():
                 ret[me] = sc_out[i]
 
+    hops = sum(piece_bytes(t) * groups for t in range(len(pieces)))
+    hops += sum(piece_bytes(number[p, "t", 0]) * groups for p in range(5) if TREE_EIGHTHS[p])
+    total = (routers - 1) * hops + (users - 1) * (2 * slot_bytes + mask_bytes)
+    drain(sent.at[0], total + size(stat_out) + size(part_out))
     handler = me // mine
     with jax.named_scope("scorewait"):
         for d in range(users):
@@ -556,24 +600,6 @@
             line = jnp.where(ranks[b] == cap, tile_in[0:1, cap * width : (cap + 1) * width], line)
         out_ref[b : b + 1, :] = jnp.where(position < fill_ref[b], line, 0.0)
 
-    for t in range(len(pieces)):
-        for j in range(1, routers):
-            x_copy(j, t, r).wait_send()
-            for i in range(1, groups):
-                y_copy(i, j, t, g).wait_send()
-    for p in range(5):
-        if TREE_EIGHTHS[p]:
-            for j in range(1, routers):
-                for i in range(groups):
-                    pair_copy(i, j, p, parity).wait_send()
-    for k in range(1, users):
-        z_copy(k, me).wait_send()
-        m_copy(k, me).wait_send()
-        relay_copy(k, h).wait_send()
-    stat_copy.wait_send()
-    for j in range(routers):
-        for c in range(2):
-            part_copy(j, c).wait_send()
     for i in range(mine):
         for e in range(heads):
 
@@ -608,10 +634,22 @@
     positions = cached * per_user
     pieces = len(ORDER)
     dma = pltpu.SemaphoreType.DMA
+    yard_bytes = 2 * (
+        (routers - 1) * (w_in.size + w_o.size)
+        + (users - 1) * (2 * CAP * (width // heads) * model + 2 * 8 * positions)
+        + 2 * rows * 128
+        + routers * half * out_cols
+    )
+    yard_rows = yard_bytes // 256 // 8 * 8
     hbm = pl.BlockSpec(memory_space=pl.ANY)
     vmem = pl.BlockSpec(memory_space=pltpu.VMEM)
-    smem = pl.BlockSpec(memory_space=pltpu.SMEM)
     scratch = [
+        pltpu.SMEM((blocks,), jnp.int32),
+        pltpu.SMEM((blocks,), jnp.int32),
+        pltpu.SMEM((blocks,), jnp.int32),
+        pltpu.VMEM(attn_gain.shape, BF16),
+        pltpu.VMEM(mlp_gain.shape, BF16),
+        pltpu.VMEM(w_two.shape, BF16),
         pltpu.VMEM((blocks, width, model), BF16),
         pltpu.VMEM((users, CAP, width // heads, model), BF16),
         pltpu.VMEM((slots, width, model), BF16),
@@ -633,29 +671,22 @@
         pltpu.VMEM((routers, half, out_cols), BF16),
         pltpu.VMEM((users // heads, 8, CAP * width), F32),
         pltpu.VMEM((users, 8, CAP * width), F32),
-        dma((6,)),
-        dma((users,)),
-        dma((users,)),
-        dma((users,)),
-        dma((users,)),
-        dma((users,)),
-        dma((users,)),
-        dma((routers, pieces)),
-        dma((routers, pieces)),
-        dma((groups, routers, pieces)),
-        dma((groups, routers, pieces)),
-        dma((groups, routers, 5)),
-        dma((groups, routers, 5)),
+        dma((8,)),
+        dma((1,)),
+        dma((users - 1,)),
+        dma((3,)),
+        dma((routers - 1, pieces)),
+        dma((groups - 1, routers - 1, 9)),
+        dma((routers - 1, 5)),
         dma((2,)),
-        dma((routers, 2)),
-        dma((routers, 2)),
         dma((users // heads, heads)),
         dma((users,)),
+        pltpu.VMEM((yard_rows, 128), BF16),
     ]
     return pl.pallas_call(
         functools.partial(scorer, sizes),
-        out_shape=jax.ShapeDtypeStruct((blocks, width), F32),
-        in_specs=[hbm, smem, smem, smem, hbm, hbm, hbm, vmem, hbm, vmem, hbm, vmem],
+        out_shape=pltpu.VMEM((blocks, width), F32),
+        in_specs=[hbm] * 12,
         out_specs=vmem,
         scratch_shapes=scratch,
         compiler_params=pltpu.CompilerParams(

time: 44.8 us -> 40.6 us (0.906)
  Pallas kernels: 43.4 us -> 39.9 us
  local copies, waits for them, and re-layouts: 1.26 us -> 0.58 us
    pallas_call x1, Pallas kernels: 43.4 us -> 39.9 us  [local(): pl.pallas_call(functools.partial(scorer, sizes), out_shape=pltpu.VMEM((bl...]
    unnamed x1, local copies, waits for them, and re-layouts: 1.26 us -> 0.58 us
where the time goes in v1:
time: 40.6 us; the launch traced here: 40.5 us
  Pallas kernels  39.9 us (98%)
  local copies, waits for them, and re-layouts  0.58 us (1%)
    pallas_call x1, Pallas kernels, local(): pl.pallas_call(functools.partial(scorer, sizes), out_shape=pltpu.VMEM((bl...  39.9 us

profile of v1, /device:TPU:0, one launch (start us, length us, event | category | flops | bytes accessed | tf_op | source)
XLA Modules:
  0.0 40.5 jit_solution(8330268863742035177)
XLA Ops:
  0.0 39.9 %shard_map.118 = f32[4,64]{1,0:T(4,128)S(1)} custom-call(bf16[4,64,1024]{2,1,0:T(8,128)(2,1)} %items_ref.1, s32[4]{0:T(128)} %bitcast.1, s32[4]{0:T(128)} %user_hbm.1, s32[4]{0:T(128)} %fill_hbm.1, bf16[2,256,512]{2,1,0:T(8,128)(2,1)} %keys_ref.1, bf16[2,256,512]{2,1,0:T(8,128)(2,1)} %values_ref.1, bf16[4,512,512]{2,1,0:T(8,128)(2,1)} %w_in_ref.1, ...), custom_call_target="tpu_custom_call" | custom-call | tf_op jit(solution)/shard_map/pallas_call | solution.py:686
  39.9 0.6 %copy.14 = f32[4,64]{1,0:T(4,128)} copy(f32[4,64]{1,0:T(4,128)S(1)} %shard_map.118) | data formatting | bytes 2048

commit v2 on v1

v2 whole, which is shorter than its diff:
```python
import functools
import math

import jax
import jax.numpy as jnp
from jax import lax
from jax.experimental import pallas as pl
from jax.experimental.pallas import tpu as pltpu
from jax.sharding import PartitionSpec as P

HEAD_DIM = 128
CAP = 2
EPSILON = 1e-05
UNIT = 512
PIECES = (
    (1, "t", 112),
    (0, "g", 80),
    (2, "t", 80),
    (0, "g", 80),
    (0, "g", 96),
    (3, "t", 64),
    (1, "g", 32),
    (3, "t", 32),
    (2, "g", 96),
    (3, "g", 64),
    (4, "g", 96),
    (4, "p", 32),
    (4, "p", 32),
    (4, "o", 192),
    (3, "o", 0),
    (2, "o", 0),
    (1, "o", 0),
    (0, "o", 0),
)
STEPS = (
    "T", "f0", "f1", "f2", "r1", "r2", "z0", "f3", "f4", "r3", "z2", "f5", "f6", "f7", "f8", "L0",
    "rA", "qA", "aA0", "aA1", "f9", "z5", "rB", "qB", "aB0", "z7", "aB1", "f10", "L1", "kA", "f11",
    "kB", "f12", "L2", "v0", "v1", "L3", "g0", "g1", "o0", "L4", "o1",
)
F32 = jnp.float32
BF16 = jnp.bfloat16
MESH = pl.DeviceIdType.MESH


def silu(v):
    return 0.5 * v * (1.0 + jnp.tanh(0.5 * v))


def plan(groups, depth, half_width):
    copies = {"t": groups * 2, "g": groups, "p": 2, "o": 1}
    lengths = [depth] * 4 + [half_width]
    filled = [0] * 5
    pieces = []
    for p, kind, share in PIECES:
        count = 0 if kind == "o" else share * lengths[p] // UNIT // 16 * 16
        pieces.append([p, kind, filled[p], count])
        filled[p] += copies[kind] * count
    for piece in pieces:
        p = piece[0]
        if piece[1] == "o":
            piece[2:] = filled[p], lengths[p] - filled[p]
            filled[p] = lengths[p]
    return pieces


def scorer(
    sizes,
    items_ref,
    owner_hbm,
    user_hbm,
    fill_hbm,
    keys_ref,
    values_ref,
    w_in_ref,
    attn_gain_hbm,
    w_o_ref,
    mlp_gain_hbm,
    w_one_ref,
    w_two_hbm,
    out_ref,
    owner_ref,
    user_ref,
    fill_ref,
    attn_gain_ref,
    mlp_gain_ref,
    w_two_ref,
    items_v,
    out_slots,
    x_all,
    mask_out,
    mask_all,
    keys_v,
    values_v,
    turned,
    gain_v,
    w_all,
    wo_all,
    w_one_v,
    q_v,
    own_v,
    att_v,
    gated_v,
    stat_out,
    stat_in,
    part_out,
    part_own,
    part_in,
    sc_out,
    ret,
    local_sem,
    sent,
    z_recv,
    group_recv,
    x_recv,
    y_recv,
    w_recv,
    st_recv,
    po_recv,
    sc_send,
    sc_recv,
    yard,
):
    groups, users, routers, heads = sizes
    g = lax.axis_index("groups")
    me = lax.axis_index("users")
    r = lax.axis_index("routers")
    h = lax.axis_index("heads")
    mate = 1 - h
    blocks, width, model = items_v.shape
    slots = x_all.shape[0]
    half_width = q_v.shape[1]
    heads_here = half_width // HEAD_DIM
    hd_all = half_width * heads
    rows = slots * width
    depth = w_all.shape[2]
    out_cols = wo_all.shape[2]
    wh = width // heads
    scale = HEAD_DIM ** (-0.5)
    positions = keys_v.shape[0] * keys_v.shape[1]
    per_user = keys_v.shape[1]

    barrier = pltpu.get_barrier_semaphore()
    count = 0
    for j in range(1, routers):
        pl.semaphore_signal(
            barrier, inc=1, device_id={"routers": lax.rem(r + j, routers)}, device_id_type=MESH
        )
        count += 1
    for i in range(1, groups):
        pl.semaphore_signal(
            barrier, inc=1, device_id={"groups": lax.rem(g + i, groups)}, device_id_type=MESH
        )
        count += 1
    pl.semaphore_signal(barrier, inc=1, device_id={"heads": mate}, device_id_type=MESH)
    count += 1
    for k in range(1, users):
        for e in range(heads):
            pl.semaphore_signal(
                barrier,
                inc=1,
                device_id={"users": lax.rem(me + k, users), "heads": e},
                device_id_type=MESH,
            )
            count += 1
    first = [
        pltpu.make_async_copy(src, dst, local_sem.at[n])
        for n, (src, dst) in enumerate(
            (
                (owner_hbm, owner_ref),
                (user_hbm, user_ref),
                (fill_hbm, fill_ref),
                (items_ref, items_v),
            )
        )
    ]
    gains = [
        pltpu.make_async_copy(src, dst, local_sem.at[4 + n])
        for n, (src, dst) in enumerate(
            (
                (attn_gain_hbm, attn_gain_ref),
                (mlp_gain_hbm, mlp_gain_ref),
                (w_two_hbm, w_two_ref),
            )
        )
    ]
    ahead = PIECES[0][0], PIECES[1][0]
    lead = [
        pltpu.make_async_copy(w_in_ref.at[p], w_all.at[p, r], local_sem.at[8 + n])
        for n, p in enumerate(ahead)
    ]
    later = [p for p in range(4) if p not in ahead]
    bulk = [
        pltpu.make_async_copy(src, dst, local_sem.at[7])
        for src, dst in [(w_in_ref.at[p], w_all.at[p, r]) for p in later]
        + [(w_o_ref, wo_all.at[r])]
    ]
    rest = [
        pltpu.make_async_copy(src, dst, local_sem.at[10])
        for src, dst in ((keys_ref, keys_v), (values_ref, values_v), (w_one_ref, w_one_v))
    ]

    def size(*refs):
        return sum(math.prod(ref.shape) * jnp.dtype(ref.dtype).itemsize for ref in refs)

    def drain(sem, amount):
        part = yard.at[pl.ds(0, amount // (yard.shape[1] * 2)), :]
        pltpu.make_async_copy(part, part, sem).wait()

    for c in lead + first + bulk:
        c.start()
    pl.semaphore_wait(barrier, count)

    pieces = plan(groups, depth, half_width)
    live = [t for t in range(len(pieces)) if pieces[t][3]]
    slot_x = {t: n for n, t in enumerate(live)}
    slot_y = {t: n + 5 for n, t in enumerate(t for t in live if pieces[t][1] == "t")}
    slot_y.update({t: pieces[t][0] for t in live if pieces[t][1] == "g"})
    parity = lax.rem(me, 2)
    pair = me + 1 - 2 * parity

    def weight_slot(owner_router, owner_group, owner_parity, t):
        p, kind, start, length = pieces[t]
        index = {
            "t": owner_group * 2 + owner_parity,
            "g": owner_group,
            "p": owner_parity,
            "o": 0,
        }[kind]
        start = start + index * length
        if kind != "o":
            start = pl.multiple_of(start, 16)
        span = pl.ds(start, length)
        if p < 4:
            return w_all.at[p, owner_router, span, :]
        return wo_all.at[owner_router, span, :]

    def piece_bytes(t):
        return size(weight_slot(0, 0, 0, t))

    def x_copy(j, t, source_router):
        spot = weight_slot(source_router, g, parity, t)
        return pltpu.make_async_remote_copy(
            src_ref=spot,
            dst_ref=spot,
            send_sem=sent.at[0],
            recv_sem=x_recv.at[j - 1, slot_x[t]],
            device_id={"routers": lax.rem(r + j, routers)},
            device_id_type=MESH,
        )

    def y_copy(i, j, t, owner_group):
        spot = weight_slot(lax.rem(r - j + routers, routers), owner_group, parity, t)
        return pltpu.make_async_remote_copy(
            src_ref=spot,
            dst_ref=spot,
            send_sem=sent.at[0],
            recv_sem=y_recv.at[i - 1, j - 1, slot_y[t]],
            device_id={"groups": lax.rem(g + i, groups)},
            device_id_type=MESH,
        )

    def pair_copy(i, j, t):
        spot = weight_slot(
            lax.rem(r - j + routers, routers), lax.rem(g - i + groups, groups), parity, t
        )
        return pltpu.make_async_remote_copy(
            src_ref=spot,
            dst_ref=spot,
            send_sem=sent.at[0],
            recv_sem=w_recv.at[j - 1, pieces[t][0]],
            device_id={"users": pair},
            device_id_type=MESH,
        )

    for n, p in enumerate(ahead):
        lead[n].wait()
        for t in (0, 1):
            if PIECES[t][0] == p and t in live:
                for j in range(1, routers):
                    x_copy(j, t, r).start()
    for c in first[:3]:
        c.wait()
    owners = [owner_ref[b] for b in range(blocks)]
    ranks = []
    for b in range(blocks):
        rank = jnp.int32(0)
        for a in range(b):
            rank = rank + jnp.where(owners[a] == owners[b], 1, 0)
        ranks.append(rank)

    def slot_source(dest, cap):
        index, user = jnp.int32(0), jnp.int32(-1)
        for b in range(blocks):
            hit = (owners[b] == dest) & (ranks[b] == cap)
            index = jnp.where(hit, b, index)
            user = jnp.where(hit, user_ref[b], user)
        return index, user

    mask_bytes = size(mask_out) // users
    slot_bytes = size(out_slots) // users
    cached = keys_v.shape[0]
    row_user = lax.broadcasted_iota(jnp.int32, (8, HEAD_DIM), 0)
    mask_copies, item_copies = {}, {}

    def across(k):
        other = me
        bit = 1
        while bit < users:
            if k & bit:
                other = other + bit - 2 * bit * lax.rem(me // bit, 2)
            bit *= 2
        return other

    def z_copy(k, source):
        return pltpu.make_async_remote_copy(
            src_ref=out_slots.at[k],
            dst_ref=x_all.at[pl.ds(source * CAP, CAP), pl.ds(pl.multiple_of(h * wh, wh), wh), :],
            send_sem=sent.at[0],
            recv_sem=z_recv.at[k - 1],
            device_id={"users": across(k)},
            device_id_type=MESH,
        )

    def m_copy(k, source):
        return pltpu.make_async_remote_copy(
            src_ref=mask_out.at[k],
            dst_ref=mask_all.at[source],
            send_sem=sent.at[0],
            recv_sem=group_recv.at[0],
            device_id={"users": across(k)},
            device_id_type=MESH,
        )

    def relay_copy(k, part):
        spot = x_all.at[
            pl.ds(across(k) * CAP, CAP), pl.ds(pl.multiple_of(part * wh, wh), wh), :
        ]
        return pltpu.make_async_remote_copy(
            src_ref=spot,
            dst_ref=spot,
            send_sem=sent.at[0],
            recv_sem=group_recv.at[2 if k == 1 else 1],
            device_id={"heads": mate},
            device_id_type=MESH,
        )

    for k in list(range(1, users)) + [0]:
        lines = jnp.zeros((8, HEAD_DIM), F32)
        for cap in range(CAP):
            user = slot_source(across(k), cap)[1]
            lines = lines + jnp.where(row_user == user + cap * cached, jnp.where(user < 0, 0.0, 1.0), 0.0)
        if k:
            mask_out[k] = lines
            m_copy(k, me).start()
        else:
            mask_all[me] = lines
    first[3].wait()
    for k in list(range(1, users)) + [0]:
        for cap in range(CAP):
            index = slot_source(across(k), cap)[0]
            if k:
                out_slots[k, cap] = items_v[index, pl.ds(pl.multiple_of(h * wh, wh), wh), :]
            else:
                x_all[me * CAP + cap] = items_v[index]
        if k:
            z_copy(k, me).start()
    drain(local_sem.at[7], size(w_o_ref) + len(later) * (size(w_in_ref) // 4))
    for t in live:
        if t > 1:
            for j in range(1, routers):
                x_copy(j, t, r).start()
    for c in rest + gains:
        c.start()

    def forward(t):
        if t not in live:
            return
        kind = pieces[t][1]
        for j in range(1, routers):
            x_copy(j, t, lax.rem(r - j + routers, routers)).wait_recv()
            if kind in "tg":
                for i in range(1, groups):
                    y_copy(i, j, t, g).start()
            if kind in "tp":
                pair_copy(0, j, t).start()

    def second(t):
        if t not in live:
            return
        for j in range(1, routers):
            for i in range(1, groups):
                y_copy(i, j, t, lax.rem(g - i + groups, groups)).wait_recv()
                pair_copy(i, j, t).start()

    def landed(p):
        mine_of = [t for t in live if pieces[t][0] == p]
        straight = sum(piece_bytes(t) for t in mine_of if pieces[t][1] == "g")
        paired = sum(
            piece_bytes(t) * (groups if pieces[t][1] == "t" else 1)
            for t in mine_of
            if pieces[t][1] in "tp"
        )
        for j in range(1, routers):
            for t in mine_of:
                if pieces[t][1] == "o":
                    x_copy(j, t, lax.rem(r - j + routers, routers)).wait_recv()
            for i in range(1, groups):
                if straight:
                    drain(y_recv.at[i - 1, j - 1, p], straight)
            if paired:
                drain(w_recv.at[j - 1, p], paired)

    tile_slots = 4
    tile = tile_slots * width
    tiles = rows // tile

    def x_tile(i):
        return x_all[pl.ds(i * tile_slots, tile_slots)].reshape(tile, model)

    def span_of(i):
        return pl.ds(pl.multiple_of(i * tile, tile), tile)

    def projected(p, i):
        x = x_tile(i)
        total = jnp.zeros((tile, half_width), F32)
        for a in range(routers):
            total = total + jnp.dot(
                x[:, a * depth : (a + 1) * depth], w_all[p, a], preferred_element_type=F32
            )
        return silu(total)

    def query(i):
        q_v[span_of(i), :] = projected(0, i).astype(BF16)

    def turn():
        gain_v[...] = mlp_gain_ref[...].astype(F32).reshape(1, -1)
        for e in range(heads_here):
            for u in range(cached):
                turned[e, u * HEAD_DIM : (u + 1) * HEAD_DIM, :] = keys_v[
                    u, :, e * HEAD_DIM : (e + 1) * HEAD_DIM
                ].T

    def attend(i, part):
        span = span_of(i)
        picks = []
        for u in range(cached):
            lines = []
            for s in range(tile_slots):
                spot = s % CAP * cached + u
                line = mask_all[i * (tile_slots // CAP) + s // CAP, spot : spot + 1, :]
                lines.append(jnp.broadcast_to(line, (width, HEAD_DIM)))
            picks.append(jnp.concatenate(lines, axis=0).astype(BF16))
        share = heads_here // 2
        for e in range(part * share, (part + 1) * share):
            cols = slice(e * HEAD_DIM, (e + 1) * HEAD_DIM)
            q = q_v[span, cols]
            raw = jnp.dot(
                jnp.concatenate([q * pick for pick in picks], axis=1),
                turned[e],
                preferred_element_type=F32,
            )
            weights = silu(raw * scale).astype(BF16)
            wide = per_user // HEAD_DIM
            weights = jnp.concatenate(
                [weights * jnp.concatenate([pick] * wide, axis=1) for pick in picks], axis=1
            )
            att_v[span, cols] = (
                jnp.dot(
                    weights,
                    values_v[:, :, cols].reshape(positions, HEAD_DIM),
                    preferred_element_type=F32,
                )
                .astype(BF16)
                .astype(F32)
            )

    def self_key(i):
        span = span_of(i)
        keys = projected(1, i)
        for e in range(heads_here):
            cols = slice(e * HEAD_DIM, (e + 1) * HEAD_DIM)
            own = jnp.sum(q_v[span, cols].astype(F32) * keys[:, cols], axis=1, keepdims=True)
            own_v[span, cols] = jnp.broadcast_to(silu(own * scale), (tile, HEAD_DIM))

    lane = lax.broadcasted_iota(jnp.int32, (tile, 128), 1)

    def self_value(i):
        span = span_of(i)
        att = att_v[span, :] + own_v[span, :] * projected(2, i)
        att_v[span, :] = att
        total = jnp.sum(att, axis=1, keepdims=True)
        square = jnp.sum(att * att, axis=1, keepdims=True)
        stat_out[span, :] = jnp.where(lane == 0, total, square)

    def gate(i):
        span = span_of(i)
        both = stat_out[span, :] + stat_in[span, :]
        mean = both[:, 0:1] / hd_all
        var = both[:, 1:2] / hd_all - mean * mean
        gated_v[span, :] = (
            (att_v[span, :] - mean)
            * lax.rsqrt(var + EPSILON)
            * attn_gain_ref[...].astype(F32).reshape(1, -1)
            * projected(3, i)
        ).astype(BF16)

    def stat_copy(i):
        return pltpu.make_async_remote_copy(
            src_ref=stat_out.at[span_of(i), :],
            dst_ref=stat_in.at[span_of(i), :],
            send_sem=sent.at[0],
            recv_sem=st_recv.at[i],
            device_id={"heads": mate},
            device_id_type=MESH,
        )

    near = me // (tile_slots // CAP)

    def over(fun, which, *args):
        if which == "A":
            fun(near, *args)
        elif tiles == 2:
            fun(1 - near, *args)
        else:

            @pl.loop(1, tiles)
            def _(n):
                fun(lax.rem(near + n, tiles), *args)

    def value(i):
        self_value(i)
        stat_copy(i).start()

    def gating(i):
        stat_copy(i).wait_recv()
        gate(i)

    def halves(fun, which):
        share = tiles // 2
        for i in range(which * share, (which + 1) * share):
            fun(i)

    half = rows // heads

    mine = users // heads
    seat, seat_mate = heads - 1 - h, heads - 1 - mate
    piece = half // 2
    source_rows = CAP * width

    def far_first(e, i, amount):
        return jnp.where(me < e * mine + mine // 2, amount - 1 - i, i)

    def part_copy(j, c):
        spot = pl.ds(pl.multiple_of(c * piece, piece), piece)
        return pltpu.make_async_remote_copy(
            src_ref=part_out.at[j, spot, :],
            dst_ref=part_in.at[j, spot, :],
            send_sem=sent.at[0],
            recv_sem=po_recv.at[c if j == 0 else 2 + c],
            device_id={"heads": mate},
            device_id_type=MESH,
        )

    def out_project(j, row_half, c, target):
        src = pl.ds(pl.multiple_of(row_half * half + c * piece, piece), piece)
        target[j, pl.ds(pl.multiple_of(c * piece, piece), piece), :] = jnp.dot(
            gated_v[src, :],
            wo_all[lax.rem(r - j + routers, routers)],
            preferred_element_type=F32,
        ).astype(target.dtype)

    def shares(j):
        for i in range(2):
            c = far_first(seat_mate, i, 2)
            out_project(j, seat_mate, c, part_out)
            part_copy(j, c).start()

    def outer(js):
        for j in js:
            shares(j)
        for j in js:
            part_own[j] = jnp.dot(
                gated_v[pl.ds(pl.multiple_of(seat * half, half), half), :],
                wo_all[lax.rem(r - j + routers, routers)],
                preferred_element_type=F32,
            )

    def step(name):
        if name == "T":
            drain(local_sem.at[10], size(keys_ref, values_ref, w_one_ref))
            for c in gains:
                c.wait()
            turn()
        elif name[0] == "f":
            forward(int(name[1:]))
        elif name[0] == "z":
            second(int(name[1:]))
        elif name[0] == "L":
            landed(int(name[1:]))
        elif name[0] == "r" and name[1] in "AB":
            if name[1] == "A":
                drain(group_recv.at[2], slot_bytes)
                drain(group_recv.at[0], (users - 1) * mask_bytes)
            else:
                drain(group_recv.at[1], (users - 2) * slot_bytes)
        elif name[0] == "r":
            for k in range(int(name[1:]), users if name == "r3" else int(name[1:]) + 1):
                z_copy(k, across(k)).wait_recv()
                relay_copy(k, h).start()
        elif name[0] == "q":
            over(query, name[1])
        elif name[0] == "a":
            over(attend, name[1], int(name[2]))
        elif name[0] == "k":
            over(self_key, name[1])
        elif name[0] == "v":
            halves(value, int(name[1]))
        elif name[0] == "g":
            halves(gating, int(name[1]))
        elif name == "o0":
            outer([0])
        else:
            outer(range(1, routers))

    for name in STEPS:
        with jax.named_scope(name):
            step(name)

    two = jnp.broadcast_to(
        w_two_ref[...].astype(F32).reshape(1, -1), (8, w_two_ref.shape[0])
    ).astype(BF16)

    def mixed(source, j):
        a = lax.rem(r - j + routers, routers)
        span = pl.ds(pl.multiple_of(source * source_rows, source_rows), source_rows)
        cols = pl.ds(pl.multiple_of(a * out_cols, out_cols), out_cols)
        x = x_all[pl.ds((seat * mine + source) * CAP, CAP), :, cols]
        x = x.reshape(source_rows, out_cols).astype(F32)
        residual = x + part_own[j, span, :] + part_in[j, span, :].astype(F32)
        square = jnp.sum(residual * residual, axis=1, keepdims=True)
        scaled = (residual * gain_v[:, cols]).astype(BF16)
        return square, jnp.dot(scaled, w_one_v[cols, :], preferred_element_type=F32)

    def score(source, i, square, total):
        for j in range(1, routers):
            more = mixed(source, j)
            square, total = square + more[0], total + more[1]
        norm = lax.rsqrt(square / model + EPSILON)
        hidden = silu(norm * total).astype(BF16)
        sc_out[i] = lax.dot_general(
            two, hidden, (((1,), (1,)), ((), ())), preferred_element_type=F32
        )

    def score_copy(i, e, owner, sem):
        return pltpu.make_async_remote_copy(
            src_ref=sc_out.at[i],
            dst_ref=ret.at[owner],
            send_sem=sc_send.at[i, e],
            recv_sem=sc_recv.at[sem],
            device_id={"users": seat * mine + far_first(seat, i, mine), "heads": e},
            device_id_type=MESH,
        )

    group = mine // 2
    early = {}
    with jax.named_scope("early"):
        for i in range(mine):
            source = far_first(seat, i, mine)
            if i % group == 0:
                drain(po_recv.at[far_first(seat, i // group, 2)], piece * out_cols * 2)
            early[i] = mixed(source, 0)
    for i in range(mine):
        source = far_first(seat, i, mine)
        if i % group == 0:
            with jax.named_scope("partwait"):
                drain(
                    po_recv.at[2 + far_first(seat, i // group, 2)],
                    (routers - 1) * piece * out_cols * 2,
                )
        with jax.named_scope("score"):
            score(source, i, *early[i])
        target = seat * mine + source
        for e in range(heads):
            itself = (target == me) & (h == e)

            @pl.when(jnp.logical_not(itself))
            def _():
                score_copy(i, e, me, me).start()

            @pl.when(itself)
            def _():
                ret[me] = sc_out[i]

    rounds = {"t": 1 + (groups - 1) + groups, "g": groups, "p": 2, "o": 1}
    hops = sum(piece_bytes(t) * rounds[pieces[t][1]] for t in live)
    total = (routers - 1) * hops + (users - 1) * (2 * slot_bytes + mask_bytes)
    drain(sent.at[0], total + size(stat_out) + size(part_out))
    handler = heads - 1 - me // mine
    with jax.named_scope("scorewait"):
        for d in range(users):

            @pl.when(jnp.logical_not((d == me) & (h == handler)))
            def _():
                score_copy(0, 0, d, d).wait_recv()

    position = lax.broadcasted_iota(jnp.int32, (1, width), 1)
    for b in range(blocks):
        tile_in = ret[owners[b]]
        line = tile_in[0:1, 0:width]
        for cap in range(1, CAP):
            line = jnp.where(ranks[b] == cap, tile_in[0:1, cap * width : (cap + 1) * width], line)
        out_ref[b : b + 1, :] = jnp.where(position < fill_ref[b], line, 0.0)

    for i in range(mine):
        for e in range(heads):

            @pl.when(jnp.logical_not((seat * mine + far_first(seat, i, mine) == me) & (h == e)))
            def _():
                score_copy(i, e, me, me).wait_send()


def local(
    sizes,
    items,
    block_owner,
    block_user,
    block_fill,
    prefix_keys,
    prefix_values,
    w_in,
    attn_gain,
    w_o,
    mlp_gain,
    w_one,
    w_two,
):
    groups, users, routers, heads = sizes
    blocks, width, model = items.shape
    projections, depth, half_width = w_in.shape
    slots = users * CAP
    rows = slots * width
    half = rows // heads
    out_cols = w_o.shape[1]
    cached, per_user, _ = prefix_keys.shape
    positions = cached * per_user
    pieces = plan(groups, depth, half_width)
    live = sum(1 for piece in pieces if piece[3])
    trees = sum(1 for piece in pieces if piece[3] and piece[1] == "t")
    dma = pltpu.SemaphoreType.DMA
    yard_bytes = 2 * (
        (routers - 1) * (w_in.size + w_o.size)
        + (users - 1) * (2 * CAP * (width // heads) * model + 2 * 8 * HEAD_DIM)
        + 2 * 2 * rows * 128
        + routers * half * out_cols
    )
    yard_rows = yard_bytes // 256 // 8 * 8
    hbm = pl.BlockSpec(memory_space=pl.ANY)
    vmem = pl.BlockSpec(memory_space=pltpu.VMEM)
    scratch = [
        pltpu.SMEM((blocks,), jnp.int32),
        pltpu.SMEM((blocks,), jnp.int32),
        pltpu.SMEM((blocks,), jnp.int32),
        pltpu.VMEM(attn_gain.shape, BF16),
        pltpu.VMEM(mlp_gain.shape, BF16),
        pltpu.VMEM(w_two.shape, BF16),
        pltpu.VMEM((blocks, width, model), BF16),
        pltpu.VMEM((users, CAP, width // heads, model), BF16),
        pltpu.VMEM((slots, width, model), BF16),
        pltpu.VMEM((users, 8, HEAD_DIM), F32),
        pltpu.VMEM((users, 8, HEAD_DIM), F32),
        pltpu.VMEM(prefix_keys.shape, BF16),
        pltpu.VMEM(prefix_values.shape, BF16),
        pltpu.VMEM((half_width // HEAD_DIM, cached * HEAD_DIM, per_user), BF16),
        pltpu.VMEM((1, model), F32),
        pltpu.VMEM((projections, routers, depth, half_width), BF16),
        pltpu.VMEM((routers, half_width, out_cols), BF16),
        pltpu.VMEM(w_one.shape, BF16),
        pltpu.VMEM((rows, half_width), BF16),
        pltpu.VMEM((rows, half_width), F32),
        pltpu.VMEM((rows, half_width), F32),
        pltpu.VMEM((rows, half_width), BF16),
        pltpu.VMEM((rows, 128), F32),
        pltpu.VMEM((rows, 128), F32),
        pltpu.VMEM((routers, half, out_cols), BF16),
        pltpu.VMEM((routers, half, out_cols), F32),
        pltpu.VMEM((routers, half, out_cols), BF16),
        pltpu.VMEM((users // heads, 8, CAP * width), F32),
        pltpu.VMEM((users, 8, CAP * width), F32),
        dma((11,)),
        dma((1,)),
        dma((users - 1,)),
        dma((3,)),
        dma((routers - 1, live)),
        dma((groups - 1, routers - 1, 5 + trees)),
        dma((routers - 1, 5)),
        dma((rows // (4 * width),)),
        dma((4,)),
        dma((users // heads, heads)),
        dma((users,)),
        pltpu.VMEM((yard_rows, 128), BF16),
    ]
    return pl.pallas_call(
        functools.partial(scorer, sizes),
        out_shape=pltpu.VMEM((blocks, width), F32),
        in_specs=[hbm] * 12,
        out_specs=vmem,
        scratch_shapes=scratch,
        compiler_params=pltpu.CompilerParams(
            collective_id=0, has_side_effects=True, vmem_limit_bytes=62 * 1024 * 1024
        ),
    )(
        items,
        block_owner.reshape(-1),
        block_user,
        block_fill,
        prefix_keys,
        prefix_values,
        w_in,
        attn_gain,
        w_o,
        mlp_gain,
        w_one,
        w_two,
    )


def solution(mesh):
    placed = (
        P(("groups", "users", "routers"), None, None),
        P(("groups", "users", "routers"), None),
        P(("groups", "users", "routers")),
        P(("groups", "users", "routers")),
        P(("groups", "users"), None, "heads"),
        P(("groups", "users"), None, "heads"),
        P(None, "routers", "heads"),
        P("heads"),
        P("heads", "routers"),
        P(),
        P(),
        P(),
    )
    sizes = tuple(mesh.shape[name] for name in ("groups", "users", "routers", "heads"))
    return jax.shard_map(
        functools.partial(local, sizes),
        mesh=mesh,
        in_specs=placed,
        out_specs=P(("groups", "users", "routers"), None),
        check_vma=False,
    )
```

time: 40.6 us -> 36.9 us (0.909)
  Pallas kernels: 39.9 us -> 36.2 us
    pallas_call x1, Pallas kernels: 39.9 us -> 36.2 us  [local(): pl.pallas_call(functools.partial(scorer, sizes), out_shape=pltpu.VMEM((bl...]
where the time goes in v2:
time: 36.9 us; the launch traced here: 36.8 us
  Pallas kernels  36.2 us (98%)
  local copies, waits for them, and re-layouts  0.58 us (2%)
    pallas_call x1, Pallas kernels, local(): pl.pallas_call(functools.partial(scorer, sizes), out_shape=pltpu.VMEM((bl...  36.2 us

profile of v2, /device:TPU:0, one launch (start us, length us, event | category | flops | bytes accessed | tf_op | source)
XLA Modules:
  0.0 36.8 jit_solution(12315737383346166957)
XLA Ops:
  0.0 36.2 %shard_map.118 = f32[4,64]{1,0:T(4,128)S(1)} custom-call(bf16[4,64,1024]{2,1,0:T(8,128)(2,1)} %items_ref.1, s32[4]{0:T(128)} %bitcast.1, s32[4]{0:T(128)} %user_hbm.1, s32[4]{0:T(128)} %fill_hbm.1, bf16[2,256,512]{2,1,0:T(8,128)(2,1)} %keys_ref.1, bf16[2,256,512]{2,1,0:T(8,128)(2,1)} %values_ref.1, bf16[4,512,512]{2,1,0:T(8,128)(2,1)} %w_in_ref.1, ...), custom_call_target="tpu_custom_call" | custom-call | tf_op jit(solution)/shard_map/pallas_call | solution.py:802
  36.2 0.6 %copy.14 = f32[4,64]{1,0:T(4,128)} copy(f32[4,64]{1,0:T(4,128)S(1)} %shard_map.118) | data formatting | bytes 2048

commit v3 on v2

--- a/solution.py
+++ b/solution.py
@@ -33,9 +33,9 @@
     (0, "o", 0),
 )
 STEPS = (
-    "T", "f0", "f1", "f2", "r1", "r2", "z0", "f3", "f4", "r3", "z2", "f5", "f6", "f7", "f8", "L0",
-    "rA", "qA", "aA0", "aA1", "f9", "z5", "rB", "qB", "aB0", "z7", "aB1", "f10", "L1", "kA", "f11",
-    "kB", "f12", "L2", "v0", "v1", "L3", "g0", "g1", "o0", "L4", "o1",
+    "T", "f0", "f1", "f2", "r1", "r2", "z0", "f3", "f4", "r3", "z2", "f5", "f6", "rA", "rB", "f7",
+    "p0", "p1", "p2", "p3", "f8", "L0", "q", "a0", "f9", "z5", "a1", "L1", "k", "z7", "f10", "f11",
+    "f12", "L2", "v", "L3", "g0", "g1", "o0", "L4", "o1",
 )
 F32 = jnp.float32
 BF16 = jnp.bfloat16
@@ -55,11 +55,14 @@
         count = 0 if kind == "o" else share * lengths[p] // UNIT // 16 * 16
         pieces.append([p, kind, filled[p], count])
         filled[p] += copies[kind] * count
-    for piece in pieces:
+    for n, piece in enumerate(pieces):
         p = piece[0]
         if piece[1] == "o":
-            piece[2:] = filled[p], lengths[p] - filled[p]
-            filled[p] = lengths[p]
+            left = lengths[p] - filled[p]
+            if any(q[:2] == piece[:2] for q in pieces[n + 1 :]):
+                left = min(left, PIECES[n][2] * lengths[p] // UNIT // 16 * 16)
+            piece[2:] = filled[p], left
+            filled[p] += left
     return pieces
 
 
@@ -93,6 +96,9 @@
     values_v,
     turned,
     gain_v,
+    pick_v,
+    gate_v,
+    pre_v,
     w_all,
     wo_all,
     w_one_v,
@@ -183,7 +189,9 @@
             )
         )
     ]
-    ahead = PIECES[0][0], PIECES[1][0]
+    order = [p for p, _, _ in PIECES]
+    ahead = list(dict.fromkeys(order))[:2]
+    opening = min(t for t, p in enumerate(order) if p not in ahead)
     lead = [
         pltpu.make_async_copy(w_in_ref.at[p], w_all.at[p, r], local_sem.at[8 + n])
         for n, p in enumerate(ahead)
@@ -272,12 +280,19 @@
             device_id_type=MESH,
         )
 
-    for n, p in enumerate(ahead):
-        lead[n].wait()
-        for t in (0, 1):
-            if PIECES[t][0] == p and t in live:
-                for j in range(1, routers):
-                    x_copy(j, t, r).start()
+    def send_x(t):
+        if t in live:
+            for j in range(1, routers):
+                x_copy(j, t, r).start()
+
+    def send_first():
+        lead[0].wait()
+        for t in range(opening):
+            if order[t] != ahead[0] and ahead[1] not in order[:t]:
+                lead[1].wait()
+            send_x(t)
+
+    send_first()
     for c in first[:3]:
         c.wait()
     owners = [owner_ref[b] for b in range(blocks)]
@@ -365,10 +380,8 @@
         if k:
             z_copy(k, me).start()
     drain(local_sem.at[7], size(w_o_ref) + len(later) * (size(w_in_ref) // 4))
-    for t in live:
-        if t > 1:
-            for j in range(1, routers):
-                x_copy(j, t, r).start()
+    for t in range(opening, len(pieces)):
+        send_x(t)
     for c in rest + gains:
         c.start()
 
@@ -412,25 +425,28 @@
 
     tile_slots = 4
     tile = tile_slots * width
-    tiles = rows // tile
-
-    def x_tile(i):
-        return x_all[pl.ds(i * tile_slots, tile_slots)].reshape(tile, model)
-
-    def span_of(i):
-        return pl.ds(pl.multiple_of(i * tile, tile), tile)
+
+    wide = 2 * tile
+
+    def wide_span(i):
+        return pl.ds(pl.multiple_of(i * wide, wide), wide)
+
+    def product(p, i, a):
+        cols = pl.ds(pl.multiple_of(a * depth, depth), depth)
+        x = x_all[pl.ds(i * 2 * tile_slots, 2 * tile_slots), :, cols]
+        return jnp.dot(x.reshape(wide, depth), w_all[p, a], preferred_element_type=F32)
+
+    def prepare(i, p):
+        pre_v[p, wide_span(i), :] = product(p, i, r)
 
     def projected(p, i):
-        x = x_tile(i)
-        total = jnp.zeros((tile, half_width), F32)
-        for a in range(routers):
-            total = total + jnp.dot(
-                x[:, a * depth : (a + 1) * depth], w_all[p, a], preferred_element_type=F32
-            )
+        total = pre_v[p, wide_span(i), :]
+        for j in range(1, routers):
+            total = total + product(p, i, lax.rem(r - j + routers, routers))
         return silu(total)
 
     def query(i):
-        q_v[span_of(i), :] = projected(0, i).astype(BF16)
+        q_v[wide_span(i), :] = projected(0, i).astype(BF16)
 
     def turn():
         gain_v[...] = mlp_gain_ref[...].astype(F32).reshape(1, -1)
@@ -440,16 +456,17 @@
                     u, :, e * HEAD_DIM : (e + 1) * HEAD_DIM
                 ].T
 
+    def picking(i):
+        for s in range(2 * tile_slots):
+            for u in range(cached):
+                spot = s % CAP * cached + u
+                line = mask_all[i * (2 * tile_slots // CAP) + s // CAP, spot : spot + 1, :]
+                rows_s = pl.ds(pl.multiple_of(i * wide + s * width, width), width)
+                pick_v[u, rows_s, :] = jnp.broadcast_to(line, (width, HEAD_DIM)).astype(BF16)
+
     def attend(i, part):
-        span = span_of(i)
-        picks = []
-        for u in range(cached):
-            lines = []
-            for s in range(tile_slots):
-                spot = s % CAP * cached + u
-                line = mask_all[i * (tile_slots // CAP) + s // CAP, spot : spot + 1, :]
-                lines.append(jnp.broadcast_to(line, (width, HEAD_DIM)))
-            picks.append(jnp.concatenate(lines, axis=0).astype(BF16))
+        span = wide_span(i)
+        picks = [pick_v[u, span, :] for u in range(cached)]
         share = heads_here // 2
         for e in range(part * share, (part + 1) * share):
             cols = slice(e * HEAD_DIM, (e + 1) * HEAD_DIM)
@@ -460,9 +477,9 @@
                 preferred_element_type=F32,
             )
             weights = silu(raw * scale).astype(BF16)
-            wide = per_user // HEAD_DIM
+            times = per_user // HEAD_DIM
             weights = jnp.concatenate(
-                [weights * jnp.concatenate([pick] * wide, axis=1) for pick in picks], axis=1
+                [weights * jnp.concatenate([pick] * times, axis=1) for pick in picks], axis=1
             )
             att_v[span, cols] = (
                 jnp.dot(
@@ -475,69 +492,58 @@
             )
 
     def self_key(i):
-        span = span_of(i)
+        span = wide_span(i)
         keys = projected(1, i)
         for e in range(heads_here):
             cols = slice(e * HEAD_DIM, (e + 1) * HEAD_DIM)
             own = jnp.sum(q_v[span, cols].astype(F32) * keys[:, cols], axis=1, keepdims=True)
-            own_v[span, cols] = jnp.broadcast_to(silu(own * scale), (tile, HEAD_DIM))
-
-    lane = lax.broadcasted_iota(jnp.int32, (tile, 128), 1)
+            own_v[span, cols] = jnp.broadcast_to(silu(own * scale), (wide, HEAD_DIM))
+
+    lane = lax.broadcasted_iota(jnp.int32, (width, 128), 1)
 
     def self_value(i):
-        span = span_of(i)
+        span = wide_span(i)
         att = att_v[span, :] + own_v[span, :] * projected(2, i)
         att_v[span, :] = att
         total = jnp.sum(att, axis=1, keepdims=True)
         square = jnp.sum(att * att, axis=1, keepdims=True)
-        stat_out[span, :] = jnp.where(lane == 0, total, square)
+        packed = jnp.zeros((width, 128), F32)
+        for b in range(wide // width):
+            part = slice(b * width, (b + 1) * width)
+            packed = jnp.where(lane == 2 * b, total[part], packed)
+            packed = jnp.where(lane == 2 * b + 1, square[part], packed)
+        stat_out[i] = packed
 
     def gate(i):
-        span = span_of(i)
-        both = stat_out[span, :] + stat_in[span, :]
-        mean = both[:, 0:1] / hd_all
-        var = both[:, 1:2] / hd_all - mean * mean
-        gated_v[span, :] = (
-            (att_v[span, :] - mean)
-            * lax.rsqrt(var + EPSILON)
-            * attn_gain_ref[...].astype(F32).reshape(1, -1)
-            * projected(3, i)
-        ).astype(BF16)
+        gate_v[wide_span(i), :] = attn_gain_ref[...].astype(F32).reshape(1, -1) * projected(3, i)
+
+    def gating(i):
+        stat_copy(i).wait_recv()
+        both = stat_out[i] + stat_in[i]
+        for b in range(wide // width):
+            span = pl.ds(pl.multiple_of(i * wide + b * width, width), width)
+            mean = both[:, 2 * b : 2 * b + 1] / hd_all
+            var = both[:, 2 * b + 1 : 2 * b + 2] / hd_all - mean * mean
+            gated_v[span, :] = (
+                (att_v[span, :] - mean) * lax.rsqrt(var + EPSILON) * gate_v[span, :]
+            ).astype(BF16)
 
     def stat_copy(i):
         return pltpu.make_async_remote_copy(
-            src_ref=stat_out.at[span_of(i), :],
-            dst_ref=stat_in.at[span_of(i), :],
+            src_ref=stat_out.at[i],
+            dst_ref=stat_in.at[i],
             send_sem=sent.at[0],
             recv_sem=st_recv.at[i],
             device_id={"heads": mate},
             device_id_type=MESH,
         )
 
-    near = me // (tile_slots // CAP)
-
-    def over(fun, which, *args):
-        if which == "A":
-            fun(near, *args)
-        elif tiles == 2:
-            fun(1 - near, *args)
-        else:
-
-            @pl.loop(1, tiles)
-            def _(n):
-                fun(lax.rem(near + n, tiles), *args)
-
     def value(i):
         self_value(i)
         stat_copy(i).start()
 
-    def gating(i):
-        stat_copy(i).wait_recv()
-        gate(i)
-
-    def halves(fun, which):
-        share = tiles // 2
-        for i in range(which * share, (which + 1) * share):
+    def whole(fun):
+        for i in range(rows // wide):
             fun(i)
 
     half = rows // heads
@@ -561,19 +567,21 @@
             device_id_type=MESH,
         )
 
-    def out_project(j, row_half, c, target):
-        src = pl.ds(pl.multiple_of(row_half * half + c * piece, piece), piece)
-        target[j, pl.ds(pl.multiple_of(c * piece, piece), piece), :] = jnp.dot(
-            gated_v[src, :],
-            wo_all[lax.rem(r - j + routers, routers)],
-            preferred_element_type=F32,
-        ).astype(target.dtype)
-
     def shares(j):
-        for i in range(2):
-            c = far_first(seat_mate, i, 2)
-            out_project(j, seat_mate, c, part_out)
-            part_copy(j, c).start()
+        pieces_of = (half,) if j == 0 else (piece, piece)
+        for i, count in enumerate(pieces_of):
+            c = 0 if j == 0 else far_first(seat_mate, i, 2)
+            start = pl.multiple_of(c * piece, piece)
+            part_out[j, pl.ds(start, count), :] = jnp.dot(
+                gated_v[pl.ds(pl.multiple_of(seat_mate * half + start, piece), count), :],
+                wo_all[lax.rem(r - j + routers, routers)],
+                preferred_element_type=F32,
+            ).astype(BF16)
+            if j:
+                part_copy(j, c).start()
+        if j == 0:
+            for i in range(2):
+                part_copy(j, far_first(seat_mate, i, 2)).start()
 
     def outer(js):
         for j in js:
@@ -601,22 +609,27 @@
             if name[1] == "A":
                 drain(group_recv.at[2], slot_bytes)
                 drain(group_recv.at[0], (users - 1) * mask_bytes)
+                whole(picking)
             else:
                 drain(group_recv.at[1], (users - 2) * slot_bytes)
         elif name[0] == "r":
             for k in range(int(name[1:]), users if name == "r3" else int(name[1:]) + 1):
                 z_copy(k, across(k)).wait_recv()
                 relay_copy(k, h).start()
+        elif name[0] == "p":
+            whole(functools.partial(prepare, p=int(name[1])))
         elif name[0] == "q":
-            over(query, name[1])
+            whole(query)
         elif name[0] == "a":
-            over(attend, name[1], int(name[2]))
+            whole(functools.partial(attend, part=int(name[1])))
         elif name[0] == "k":
-            over(self_key, name[1])
+            whole(self_key)
         elif name[0] == "v":
-            halves(value, int(name[1]))
-        elif name[0] == "g":
-            halves(gating, int(name[1]))
+            whole(value)
+        elif name == "g0":
+            whole(gate)
+        elif name == "g1":
+            whole(gating)
         elif name == "o0":
             outer([0])
         else:
@@ -772,6 +785,9 @@
         pltpu.VMEM(prefix_values.shape, BF16),
         pltpu.VMEM((half_width // HEAD_DIM, cached * HEAD_DIM, per_user), BF16),
         pltpu.VMEM((1, model), F32),
+        pltpu.VMEM((cached, rows, HEAD_DIM), BF16),
+        pltpu.VMEM((rows, half_width), F32),
+        pltpu.VMEM((projections, rows, half_width), F32),
         pltpu.VMEM((projections, routers, depth, half_width), BF16),
         pltpu.VMEM((routers, half_width, out_cols), BF16),
         pltpu.VMEM(w_one.shape, BF16),
@@ -779,8 +795,8 @@
         pltpu.VMEM((rows, half_width), F32),
         pltpu.VMEM((rows, half_width), F32),
         pltpu.VMEM((rows, half_width), BF16),
-        pltpu.VMEM((rows, 128), F32),
-        pltpu.VMEM((rows, 128), F32),
+        pltpu.VMEM((rows // (8 * width), width, 128), F32),
+        pltpu.VMEM((rows // (8 * width), width, 128), F32),
         pltpu.VMEM((routers, half, out_cols), BF16),
         pltpu.VMEM((routers, half, out_cols), F32),
         pltpu.VMEM((routers, half, out_cols), BF16),
@@ -793,7 +809,7 @@
         dma((routers - 1, live)),
         dma((groups - 1, routers - 1, 5 + trees)),
         dma((routers - 1, 5)),
-        dma((rows // (4 * width),)),
+        dma((rows // (8 * width),)),
         dma((4,)),
         dma((users // heads, heads)),
         dma((users,)),

time: 36.9 us -> 36.7 us (level)
  no operation moved by 1% of the time
where the time goes in v3:
time: 36.7 us; the launch traced here: 36.5 us
  Pallas kernels  35.9 us (98%)
  local copies, waits for them, and re-layouts  0.58 us (2%)
    pallas_call x1, Pallas kernels, local(): pl.pallas_call(functools.partial(scorer, sizes), out_shape=pltpu.VMEM((bl...  35.9 us

profile of v3, /device:TPU:0, one launch (start us, length us, event | category | flops | bytes accessed | tf_op | source)
XLA Modules:
  0.0 36.5 jit_solution(10908726354371274143)
XLA Ops:
  0.0 35.9 %shard_map.118 = f32[4,64]{1,0:T(4,128)S(1)} custom-call(bf16[4,64,1024]{2,1,0:T(8,128)(2,1)} %items_ref.1, s32[4]{0:T(128)} %bitcast.1, s32[4]{0:T(128)} %user_hbm.1, s32[4]{0:T(128)} %fill_hbm.1, bf16[2,256,512]{2,1,0:T(8,128)(2,1)} %keys_ref.1, bf16[2,256,512]{2,1,0:T(8,128)(2,1)} %values_ref.1, bf16[4,512,512]{2,1,0:T(8,128)(2,1)} %w_in_ref.1, ...), custom_call_target="tpu_custom_call" | custom-call | tf_op jit(solution)/shard_map/pallas_call | solution.py:818
  35.9 0.6 %copy.14 = f32[4,64]{1,0:T(4,128)} copy(f32[4,64]{1,0:T(4,128)S(1)} %shard_map.118) | data formatting | bytes 2048

commit v4 on v3

--- a/solution.py
+++ b/solution.py
@@ -24,9 +24,9 @@
     (2, "g", 96),
     (3, "g", 64),
     (4, "g", 96),
+    (4, "p", 48),
     (4, "p", 32),
-    (4, "p", 32),
-    (4, "o", 192),
+    (4, "o", 160),
     (3, "o", 0),
     (2, "o", 0),
     (1, "o", 0),

time: 36.7 us -> 36.5 us (level)
  no operation moved by 1% of the time
where the time goes in v4:
time: 36.5 us; the launch traced here: 36.4 us
  Pallas kernels  35.8 us (98%)
  local copies, waits for them, and re-layouts  0.58 us (2%)
    pallas_call x1, Pallas kernels, local(): pl.pallas_call(functools.partial(scorer, sizes), out_shape=pltpu.VMEM((bl...  35.8 us

profile of v4, /device:TPU:0, one launch (start us, length us, event | category | flops | bytes accessed | tf_op | source)
XLA Modules:
  0.0 36.4 jit_solution(18382026402615406074)
XLA Ops:
  0.0 35.8 %shard_map.118 = f32[4,64]{1,0:T(4,128)S(1)} custom-call(bf16[4,64,1024]{2,1,0:T(8,128)(2,1)} %items_ref.1, s32[4]{0:T(128)} %bitcast.1, s32[4]{0:T(128)} %user_hbm.1, s32[4]{0:T(128)} %fill_hbm.1, bf16[2,256,512]{2,1,0:T(8,128)(2,1)} %keys_ref.1, bf16[2,256,512]{2,1,0:T(8,128)(2,1)} %values_ref.1, bf16[4,512,512]{2,1,0:T(8,128)(2,1)} %w_in_ref.1, ...), custom_call_target="tpu_custom_call" | custom-call | tf_op jit(solution)/shard_map/pallas_call | solution.py:818
  35.8 0.6 %copy.14 = f32[4,64]{1,0:T(4,128)} copy(f32[4,64]{1,0:T(4,128)S(1)} %shard_map.118) | data formatting | bytes 2048

commit v5 on v4

--- a/solution.py
+++ b/solution.py
@@ -668,8 +668,8 @@
         return pltpu.make_async_remote_copy(
             src_ref=sc_out.at[i],
             dst_ref=ret.at[owner],
-            send_sem=sc_send.at[i, e],
-            recv_sem=sc_recv.at[sem],
+            send_sem=sc_send.at[0],
+            recv_sem=sc_recv.at[0],
             device_id={"users": seat * mine + far_first(seat, i, mine), "heads": e},
             device_id_type=MESH,
         )
@@ -709,12 +709,14 @@
     total = (routers - 1) * hops + (users - 1) * (2 * slot_bytes + mask_bytes)
     drain(sent.at[0], total + size(stat_out) + size(part_out))
     handler = heads - 1 - me // mine
-    with jax.named_scope("scorewait"):
-        for d in range(users):
-
-            @pl.when(jnp.logical_not((d == me) & (h == handler)))
-            def _():
-                score_copy(0, 0, d, d).wait_recv()
+    score_bytes = size(ret) // users
+
+    def gather(less):
+        drain(sc_recv.at[0], (users - less) * score_bytes)
+        drain(sc_send.at[0], (users - less) * score_bytes)
+
+    pl.when(h == handler)(functools.partial(gather, 1))
+    pl.when(h != handler)(functools.partial(gather, 0))
 
     position = lax.broadcasted_iota(jnp.int32, (1, width), 1)
     for b in range(blocks):
@@ -723,13 +725,6 @@
         for cap in range(1, CAP):
             line = jnp.where(ranks[b] == cap, tile_in[0:1, cap * width : (cap + 1) * width], line)
         out_ref[b : b + 1, :] = jnp.where(position < fill_ref[b], line, 0.0)
-
-    for i in range(mine):
-        for e in range(heads):
-
-            @pl.when(jnp.logical_not((seat * mine + far_first(seat, i, mine) == me) & (h == e)))
-            def _():
-                score_copy(i, e, me, me).wait_send()
 
 
 def local(
@@ -811,8 +806,8 @@
         dma((routers - 1, 5)),
         dma((rows // (8 * width),)),
         dma((4,)),
-        dma((users // heads, heads)),
-        dma((users,)),
+        dma((1,)),
+        dma((1,)),
         pltpu.VMEM((yard_rows, 128), BF16),
     ]
     return pl.pallas_call(

time: 36.5 us -> 36.4 us (level)
  no operation moved by 1% of the time
where the time goes in v5:
time: 36.4 us; the launch traced here: 36.3 us
  Pallas kernels  35.7 us (98%)
  local copies, waits for them, and re-layouts  0.58 us (2%)
    pallas_call x1, Pallas kernels, local(): pl.pallas_call(functools.partial(scorer, sizes), out_shape=pltpu.VMEM((bl...  35.7 us

profile of v5, /device:TPU:0, one launch (start us, length us, event | category | flops | bytes accessed | tf_op | source)
XLA Modules:
  0.0 36.3 jit_solution(17382430305798175590)
XLA Ops:
  0.0 35.7 %shard_map.118 = f32[4,64]{1,0:T(4,128)S(1)} custom-call(bf16[4,64,1024]{2,1,0:T(8,128)(2,1)} %items_ref.1, s32[4]{0:T(128)} %bitcast.1, s32[4]{0:T(128)} %user_hbm.1, s32[4]{0:T(128)} %fill_hbm.1, bf16[2,256,512]{2,1,0:T(8,128)(2,1)} %keys_ref.1, bf16[2,256,512]{2,1,0:T(8,128)(2,1)} %values_ref.1, bf16[4,512,512]{2,1,0:T(8,128)(2,1)} %w_in_ref.1, ...), custom_call_target="tpu_custom_call" | custom-call | tf_op jit(solution)/shard_map/pallas_call | solution.py:813
  35.7 0.6 %copy.14 = f32[4,64]{1,0:T(4,128)} copy(f32[4,64]{1,0:T(4,128)S(1)} %shard_map.118) | data formatting | bytes 2048
